TPU v7x, 256 devices: a whole 4x4x8 slice. The times are simulated.
256 devices in a mesh: row: 2 (over core), col: 4 (over x), depth: 32 (over z, y).
Axes of the slice: x: 4, y: 4, z: 8, core: 2. Of those that a mesh axis runs over, the one named last changes fastest.
Arguments:
- a_tile: float32 [2048, 2048], P('row', 'col'), as said below
- panels: float32 [2048, 32768], P('row', 'depth'), as said below
Outputs:
- trailing: float32 [2048, 2048], P(('row', 'depth'), 'col')
- new_panel: float32 [2048, 512], P(('row', 'col'))
- diag_norm: float32 [1], replicated
Inputs may be any that keep to these rules, and one draw needn't show every extreme that they name: symmetric; a_tile - panels panels^T is positive definite with a large positive diagonal. `panels`: real-valued entries of full rank.
All inputs are finite; a program needn't handle non-finite values.
Results may differ from a plain program's by a relative error of at most 0.00015.
Values sent between devices are 32-bit elements; how exact they have to be, the bound alone decides.
No kernel may reach another device: no remote copies, remote signals or barrier semaphores. Data moves between devices by JAX's collectives and lax.ppermute only.
A program may use at most 64 MiB of HBM per device.

v0:
```python
import jax
import jax.numpy as jnp
from jax import lax
from jax.sharding import Mesh
from jax.sharding import PartitionSpec as P

PB = 512
DEPTH = ("depth_0", "depth_1")
ROW_COL_DEPTH = ("row", "col", "depth_0", "depth_1")
ROW_DEPTH = ("row", "depth_0", "depth_1")


def broadcast(value, axis, root):
    return lax.dynamic_index_in_dim(lax.all_gather(value, axis), root, 0, keepdims=False)


def split_up(value, dim, size):
    dims = value.shape
    pieces = value.reshape(*dims[:dim], size, dims[dim] // size, *dims[dim + 1 :])
    return jnp.moveaxis(pieces, dim, 0)


def sum_at_owner(value, axis, dim):
    pieces = split_up(value, dim, lax.axis_size(axis))
    arrived = lax.all_to_all(pieces, axis, split_axis=0, concat_axis=0, tiled=True)
    return arrived.sum(axis=0)


def from_everyone(value, axis):
    size = lax.axis_size(axis)
    return lax.all_to_all(
        jnp.broadcast_to(value[None], (size, *value.shape)), axis, 0, 0, tiled=True
    )


def joined_along(pieces, dim):
    pieces = jnp.moveaxis(pieces, 0, dim)
    dims = pieces.shape
    return pieces.reshape(*dims[:dim], dims[dim] * dims[dim + 1], *dims[dim + 2 :])


def gathered_copies(value, axis, dim):
    pieces = from_everyone(value, axis)
    return joined_along(pieces, dim)


def over_axes(value, axes):
    for axis in axes:
        value = lax.psum(value, axis)
    return value


def outer_rows(left, right):
    return lax.dot_general(
        left,
        right,
        (((1,), (1,)), ((), ())),
        precision=lax.Precision.HIGHEST,
        preferred_element_type=jnp.float32,
    )


def local(a_tile, panels):
    tile_rows, tile_cols = a_tile.shape
    depth_count = lax.axis_size(DEPTH)
    row_index = lax.axis_index("row")
    col_index = lax.axis_index("col")
    depth_index = lax.axis_index(DEPTH)
    first = col_index * tile_cols
    piece_rows = min(tile_rows, tile_cols)
    start = first + 0
    owner = start // tile_rows
    offset = start % tile_rows
    sent = lax.dynamic_slice_in_dim(panels, offset, piece_rows, 0)
    pieces = broadcast(sent, "row", owner)
    keep_base = depth_index == 0
    share_rows = tile_rows // depth_count
    trailing = sum_at_owner(
        jnp.where(keep_base, a_tile, 0.0) - outer_rows(panels, pieces), DEPTH, 0
    )
    panel_block = gathered_copies(trailing, DEPTH, 0)
    diag_block = broadcast(panel_block[:PB], "row", 0)
    factor = jnp.linalg.cholesky(diag_block)
    solved = jax.scipy.linalg.solve_triangular(factor, panel_block.T, lower=True).T
    col_share = tile_rows // lax.axis_size("col")
    received = lax.all_to_all(solved, "col", split_axis=0, concat_axis=0, tiled=True)
    new_panel = received[:col_share]
    rows_global = (
        row_index * tile_rows
        + depth_index * share_rows
        + jnp.arange(share_rows, dtype=jnp.int32)[:, None]
    )
    cols_global = first + jnp.arange(tile_cols, dtype=jnp.int32)[None, :]
    squares = jnp.sum(jnp.where(rows_global == cols_global, trailing * trailing, 0.0))
    total = over_axes(squares, ROW_COL_DEPTH)
    order = tile_cols * lax.axis_size("col")
    diag_norm = jnp.sqrt(total / order).reshape(1)
    return (trailing, new_panel, diag_norm)


def solution(mesh):
    finer = Mesh(
        mesh.devices.reshape(mesh.shape["row"], mesh.shape["col"], 8, 4),
        ("row", "col", "depth_0", "depth_1"),
    )
    in_specs = (P("row", "col"), P("row", DEPTH))
    out_specs = (P(ROW_DEPTH, "col"), P(("row", "col"), None), P())
    return jax.shard_map(local, mesh=finer, in_specs=in_specs, out_specs=out_specs, check_vma=False)
```

profile of v0, /device:TPU:2, one launch (start us, length us, event | category | flops | bytes accessed | tf_op | source)
XLA Modules:
  0.0 399.6 jit_solution(11369254155809426649)
XLA Ops:
  7.2 3.2 constant_dynamic-slice_fusion.1
  12.4 20.1 %all-gather.6.cloned.1.call-done = f32[1024,1024]{1,0:T(8,128)} async-done(((f32[512,1024]{1,0:T(8,128)}), f32[1024,1024]{1,0:T(8,128)}) %all-gather.6.cloned.1.call-update) | async-done | bytes 4194320 | tf_op jit(solution)/shard_map/all_gather | solution.py:14
  32.5 10.3 %bitcast_subtract_fusion = f32[1024,512]{0,1:T(8,128)} fusion(f32[1024,512]{0,1:T(8,128)S(1)} %copy.14, f32[1024,1024]{1,0:T(8,128)} %param.3, f32[2,512,1024]{2,1,0:T(8,128)} %bitcast.78, s32[]{:T(128)S(6)} %select_n.41, pred[]{:T(512)S(6)} %eq.18), kind=kOutput, calls=%fused_computation.3 | convolution fusion | flops 6443499520 | bytes 10485765 | tf_op jit(solution)/shard_map/dot_general | solution.py:54
  44.8 60.7 %all_to_all.19 = f32[32,32,512]{2,1,0:T(8,128)} all-to-all(f32[32,32,512]{2,1,0:T(8,128)S(1)} %bitcast.76), channel_id=1, replica_groups=mesh['row'=2,'col'=4,'depth_0'=8,'depth_1'=4] {'depth_0','depth_1'}, dimensions={0} | all-to-all | bytes 4194304 | tf_op jit(solution)/shard_map/all_to_all | solution.py:25
  107.5 54.9 %all_to_all.20 = f32[32,32,512]{2,1,0:T(8,128)S(1)} all-to-all(f32[32,32,512]{2,1,0:T(8,128)S(1)} %broadcast_in_dim.19), channel_id=1, replica_groups=mesh['row'=2,'col'=4,'depth_0'=8,'depth_1'=4] {'depth_0','depth_1'}, dimensions={0} | all-to-all | bytes 4194304 | tf_op jit(solution)/shard_map/all_to_all | solution.py:31
  165.6 11.0 %all-gather.4.cloned.1.call-done = f32[2,512,512]{2,1,0:T(8,128)} async-done(((f32[1,512,512]{2,1,0:T(8,128)}), f32[2,512,512]{2,1,0:T(8,128)}) %all-gather.4.cloned.1.call-update) | async-done | bytes 2097168 | tf_op jit(solution)/shard_map/all_gather | solution.py:14
  179.7 11.7 %cholesky.104 = f32[128,128]{1,0:T(8,128)S(1)} custom-call(f32[128,128]{1,0:T(8,128)S(1)} %cholesky.266), custom_call_target="Cholesky" | custom-call | tf_op jit(solution)/shard_map/jit(cholesky)/cholesky | solution.py:83
  191.5 9.8 %custom-call.31 = f32[1,128,128]{1,2,0:T(8,128)S(1)} custom-call(f32[1,128,128]{2,1,0:T(8,128)S(1)} %get-tuple-element.30), custom_call_target="InvertDiagBlocksLowerTriangular" | custom-call | tf_op jit(solution)/shard_map/jit(cholesky)/cholesky | solution.py:83
  202.0 11.7 %cholesky.217 = f32[128,128]{1,0:T(8,128)S(1)} custom-call(f32[128,128]{1,0:T(8,128)S(1)} %cholesky.270), custom_call_target="Cholesky" | custom-call | tf_op jit(solution)/shard_map/jit(cholesky)/cholesky | solution.py:83
  213.8 10.0 %custom-call.32 = f32[1,128,128]{1,2,0:T(8,128)S(1)} custom-call(f32[1,128,128]{2,1,0:T(8,128)S(1)} %get-tuple-element.27), custom_call_target="InvertDiagBlocksLowerTriangular" | custom-call | tf_op jit(solution)/shard_map/jit(cholesky)/cholesky | solution.py:83
  224.5 11.7 %cholesky.238 = f32[128,128]{1,0:T(8,128)S(1)} custom-call(f32[128,128]{1,0:T(8,128)S(1)} %cholesky.275), custom_call_target="Cholesky" | custom-call | tf_op jit(solution)/shard_map/jit(cholesky)/cholesky | solution.py:83
  236.8 9.8 %custom-call.33 = f32[1,128,128]{1,2,0:T(8,128)S(1)} custom-call(f32[1,128,128]{2,1,0:T(8,128)S(1)} %get-tuple-element.24), custom_call_target="InvertDiagBlocksLowerTriangular" | custom-call | tf_op jit(solution)/shard_map/jit(cholesky)/cholesky | solution.py:83
  248.1 11.7 %cholesky.255 = f32[128,128]{1,0:T(8,128)S(1)} custom-call(f32[128,128]{1,0:T(8,128)S(1)} %convolution_subtract_fusion.4), custom_call_target="Cholesky" | custom-call | tf_op jit(solution)/shard_map/jit(cholesky)/cholesky | solution.py:83
  264.9 13.5 %while.1 = (s32[]{:T(128)}, f32[512,512]{1,0:T(8,128)}, s32[4,2]{0,1:T(2,128)S(1)}, f32[4,128,128]{2,1,0:T(8,128)}, s32[]{:T(128)}) while((s32[]{:T(128)}, f32[512,512]{1,0:T(8,128)}, s32[4,2]{0,1:T(2,128)S(1)}, f32[4,128,128]{2,1,0:T(8,128)}, s32[]{:T(128)}) %tuple.31), condition=%wide.while_cond, body=%wide.while_body.sunk | while | flops 2 | bytes 132705 | solution.py:84
  265.5 2.8 bitcast_dynamic-update-slice_fusion.2
  268.9 2.8 bitcast_dynamic-update-slice_fusion.2
  272.3 2.8 bitcast_dynamic-update-slice_fusion.2
  275.7 2.7 bitcast_dynamic-update-slice_fusion.2
  278.4 40.1 %custom-call.34 = f32[4,128,128]{1,2,0:T(8,128)S(1)} custom-call(f32[4,128,128]{2,1,0:T(8,128)} %get-tuple-element.10), custom_call_target="InvertDiagBlocksLowerTriangular" | custom-call | tf_op jit(solution)/shard_map/jit(_solve_triangular)/triangular_solve | solution.py:84
  328.2 4.8 %all-to-all-start.2 = ((f32[4,256,512]{2,1,0:T(8,128)}), f32[4,256,512]{2,1,0:T(8,128)S(1)}, u32[]{:S(2)}, u32[]{:S(2)}) async-start(f32[4,256,512]{2,1,0:T(8,128)} %bitcast.20), calls=%async_computation.2 | async-start | bytes 4194304 | tf_op jit(solution)/shard_map/all_to_all | solution.py:86
  333.7 3.1 psum.28
  336.8 23.7 %psum.29 = f32[]{:T(128)} all-reduce(f32[]{:T(128)} %psum.28), channel_id=1, replica_groups=mesh['row'=2,'col'=4,'depth_0'=8,'depth_1'=4] {'col'}, use_global_device_ids=true, to_apply=%region_11.12 | all-reduce | flops 1 | bytes 8 | tf_op jit(solution)/shard_map/psum | solution.py:49
  360.5 18.1 %psum.30 = f32[]{:T(128)} all-reduce(f32[]{:T(128)} %psum.29), channel_id=1, replica_groups=mesh['row'=2,'col'=4,'depth_0'=8,'depth_1'=4] {'depth_0'}, use_global_device_ids=true, to_apply=%region_12.13 | all-reduce | flops 1 | bytes 8 | tf_op jit(solution)/shard_map/psum | solution.py:49
  378.6 11.1 %psum.31 = f32[]{:T(128)} all-reduce(f32[]{:T(128)} %psum.30), channel_id=1, replica_groups=mesh['row'=2,'col'=4,'depth_0'=8,'depth_1'=4] {'depth_1'}, use_global_device_ids=true, to_apply=%region_13.14 | all-reduce | flops 1 | bytes 8 | tf_op jit(solution)/shard_map/psum | solution.py:49
  (63 shorter events, 31.9 us)
Async XLA Ops:
  7.2 25.4 %all-gather.6.cloned.1.call-start = ((), (), s32[]{:S(2)}) async-start(), calls=%async_computation.4 | async-start | bytes 6291456 | tf_op jit(solution)/shard_map/all_gather | solution.py:14
  10.4 166.2 %all-gather.4.cloned.1.call-start = ((), (), s32[]{:S(2)}) async-start(), calls=%async_computation.3 | async-start | bytes 3145728 | tf_op jit(solution)/shard_map/all_gather | solution.py:14
  107.2 225.8 %copy-start.2 = (f32[32,512]{1,0:T(8,128)}, f32[32,512]{1,0:T(8,128)S(1)}, u32[]{:S(2)}) copy-start(f32[32,512]{1,0:T(8,128)S(1)} %reduce_sum.18) | copy-start | bytes 196612
  176.6 1.2 slice-start
  179.6 44.4 %copy-start.1 = (f32[512,512]{1,0:T(8,128)}, f32[512,512]{1,0:T(8,128)S(1)}, u32[]{:S(2)}) copy-start(f32[512,512]{1,0:T(8,128)S(1)} %fusion.17) | copy-start | bytes 3145732
  224.4 94.1 %copy-start = (f32[1024,512]{0,1:T(8,128)S(1)}, f32[1024,512]{0,1:T(8,128)}, u32[]{:S(2)}) copy-start(f32[1024,512]{0,1:T(8,128)} %copy.18) | copy-start | bytes 6291460
  328.2 62.1 %all-to-all-start.2 = ((f32[4,256,512]{2,1,0:T(8,128)}), f32[4,256,512]{2,1,0:T(8,128)S(1)}, u32[]{:S(2)}, u32[]{:S(2)}) async-start(f32[4,256,512]{2,1,0:T(8,128)} %bitcast.20), calls=%async_computation.2 | async-start | bytes 4194304 | tf_op jit(solution)/shard_map/all_to_all | solution.py:86
Sparse Core Ops, SparseCore 0:
  10.6 21.9 all-gather.5
  163.6 12.9 all-gather.3
where the time goes:
time: 405 us; the launch traced here: 400 us
  blocking collectives  172 us (42%)
  other arithmetic  124 us (31%)
  waiting for transfers between devices  31.2 us (8%)
  local copies, waits for them, and re-layouts  28.3 us (7%)
  matrix products  20.6 us (5%)
  between operations  19 us (5%)
  starting transfers between devices  4.87 us (1%)
    another operation x14, other arithmetic, local(): factor = jnp.linalg.cholesky(diag_block)  78.5 us
    all_to_all x1, blocking collectives, sum_at_owner(): lax.all_to_all(pieces, axis, split_axis=0, concat_axis=0, tiled=True)  60.7 us
    psum x4, blocking collectives, over_axes(): value = lax.psum(value, axis)  55.9 us
    all_to_all x1, blocking collectives, from_everyone(): lax.all_to_all(jnp.broadcast_to(value[None], (size, *value.shape)), axis,...  54.9 us
    another operation x3, other arithmetic, local(): jax.scipy.linalg.solve_triangular(factor, panel_block.T, lower=True)  41.5 us
    all_gather x2, waiting for transfers between devices, broadcast(): lax.all_gather(value, axis)  31.1 us
    another operation x12, local copies, waits for them, and re-layouts  13.5 us
    dot_general x1, matrix products, outer_rows(): lax.dot_general(left, right, (((1,), (1,)), ((), ())), precision=lax.Prec...  10.3 us
  transfers between devices with their start and end apart: 3, of which 2 were waited for; matrix products, arithmetic and copies ran while one was open for 1% of the time, Pallas kernels for 0%

commit v1 on v0

v1 whole, which is shorter than its diff:
```python
import jax
import jax.numpy as jnp
from jax import lax
from jax.experimental import pallas as pl
from jax.experimental.pallas import tpu as pltpu
from jax.sharding import Mesh
from jax.sharding import PartitionSpec as P

PB = 512
LANES = 128
SUBLANES = 8
GROUPS = LANES // SUBLANES
BLOCKS = PB // LANES
PAIRS = BLOCKS * (BLOCKS + 1) // 2
DEPTH = ("depth_0", "depth_1")
ROW_DEPTH = ("row", "depth_0", "depth_1")
F32 = jnp.float32


def times_transposed(left, right):
    return lax.dot_general(
        left,
        right,
        (((1,), (1,)), ((), ())),
        precision=lax.Precision.HIGHEST,
        preferred_element_type=F32,
    )


def pair(i, j):
    return i * (i + 1) // 2 + j


def inverse_factor(load, store):
    lane = lax.broadcasted_iota(jnp.int32, (SUBLANES, LANES), 1)
    sub = lax.broadcasted_iota(jnp.int32, (SUBLANES, LANES), 0)
    whole = (SUBLANES, LANES)
    rows = [load(h) for h in range(GROUPS)]
    for g in range(GROUPS):
        first = SUBLANES * g
        cols = {
            h: [
                jnp.broadcast_to(rows[h][:, first + j : first + j + 1], whole)
                for j in range(SUBLANES)
            ]
            for h in range(g, GROUPS)
        }
        inside = (lane >= first) & (lane < first + SUBLANES)
        rows[g] = jnp.where(inside, jnp.where(lane - first == sub, 1.0, 0.0), rows[g])
        for h in range(g + 1, GROUPS):
            rows[h] = jnp.where(inside, 0.0, rows[h])
        done = jnp.zeros(whole, F32)
        for j in range(SUBLANES):
            scale = lax.rsqrt(jnp.broadcast_to(cols[g][j][j : j + 1], whole))
            row = jnp.broadcast_to(rows[g][j : j + 1], whole) * scale
            done = jnp.where(sub == j, row, done)
            own = cols[g][j] * scale
            spread = {
                k: jnp.broadcast_to(own[k : k + 1], whole) for k in range(j + 1, SUBLANES)
            }
            for k in spread:
                cols[g][k] = cols[g][k] - own * spread[k]
            rows[g] = rows[g] - jnp.where(sub > j, own, 0.0) * row
            for h in range(g + 1, GROUPS):
                below = cols[h][j] * scale
                rows[h] = rows[h] - below * row
                for k in spread:
                    cols[h][k] = cols[h][k] - below * spread[k]
        store(g, jnp.where(lane <= first + sub, done, 0.0))


def solve_kernel(top_ref, mine_ref, other_ref, c_ref, x_ref, w, inv_ref):
    pieces, per_piece = mine_ref.shape[0], PAIRS * GROUPS // mine_ref.shape[0]
    top = top_ref[0] == 0
    for ref, mine in ((mine_ref, top), (other_ref, jnp.logical_not(top))):

        @pl.when(mine)
        def _(ref=ref):
            for t in range(pieces * per_piece):
                b, h = t // GROUPS, t % GROUPS
                w[b, SUBLANES * h : SUBLANES * (h + 1)] = ref[t // per_piece, t % per_piece]

    x_ref[...] = c_ref[...]

    def step(b, carry):
        diag = (b * (b + 3)) // 2

        def load(h):
            return w[diag, SUBLANES * h : SUBLANES * (h + 1)]

        def store(h, value):
            inv_ref[SUBLANES * h : SUBLANES * (h + 1)] = value

        inverse_factor(load, store)
        for s in range(BLOCKS):

            @pl.when(b == s)
            def _(s=s):
                inv = inv_ref[...]
                here = slice(LANES * s, LANES * (s + 1))
                for i in range(s + 1, BLOCKS):
                    w[pair(i, s)] = times_transposed(w[pair(i, s)], inv)
                x = times_transposed(x_ref[:, here], inv)
                x_ref[:, here] = x
                for j in range(s + 1, BLOCKS):
                    there = slice(LANES * j, LANES * (j + 1))
                    for i in range(j, BLOCKS):
                        w[pair(i, j)] = w[pair(i, j)] - times_transposed(w[pair(i, s)], w[pair(j, s)])
                    x_ref[:, there] = x_ref[:, there] - times_transposed(x, w[pair(j, s)])

        return carry

    lax.fori_loop(0, BLOCKS, step, 0)


def solve(row_index, mine, other, c_rows):
    vmem = pl.BlockSpec(memory_space=pltpu.VMEM)
    return pl.pallas_call(
        solve_kernel,
        out_shape=jax.ShapeDtypeStruct(c_rows.shape, F32),
        in_specs=[pl.BlockSpec(memory_space=pltpu.SMEM), vmem, vmem, vmem],
        out_specs=vmem,
        scratch_shapes=[
            pltpu.VMEM((PAIRS, LANES, LANES), F32),
            pltpu.VMEM((LANES, LANES), F32),
        ],
        cost_estimate=pl.CostEstimate(flops=20_000_000_000, bytes_accessed=3_000_000, transcendentals=512),
        name="panel_solve",
    )(row_index.reshape(1).astype(jnp.int32), mine, other, c_rows)


def exchange(pieces, axis):
    return lax.all_to_all(pieces, axis, split_axis=0, concat_axis=0, tiled=True)


def to_everyone(value, axis):
    size = lax.axis_size(axis)
    return exchange(jnp.broadcast_to(value[None], (size, *value.shape)), axis)


def packed(square):
    return jnp.concatenate(
        [
            square[LANES * i : LANES * (i + 1), LANES * j : LANES * (j + 1)]
            for i in range(BLOCKS)
            for j in range(i + 1)
        ]
    )


def first_row_of_tile(values):
    n, k = values.shape
    return jnp.pad(values[:, None, None, :], ((0, 0), (0, 0), (0, SUBLANES - 1), (0, LANES - k)))


def local(a_tile, panels):
    tile_rows, tile_cols = a_tile.shape
    rows, cols = lax.axis_size("row"), lax.axis_size("col")
    depth = lax.axis_size(DEPTH)
    z_size, y_size = lax.axis_size("depth_0"), lax.axis_size("depth_1")
    r, c, d = lax.axis_index("row"), lax.axis_index("col"), lax.axis_index(DEPTH)
    share = tile_rows // depth
    c_rows = tile_rows // cols
    c_share = c_rows // depth
    tiles = PAIRS * GROUPS // depth

    a_share = lax.dynamic_slice_in_dim(a_tile, d * share, share, 0)
    a_diag = lax.dynamic_slice_in_dim(packed(a_tile[:PB]), d * tiles * SUBLANES, tiles * SUBLANES, 0)
    a_panel = lax.dynamic_slice_in_dim(a_tile.reshape(cols, c_rows, tile_cols), d * c_share, c_share, 1)
    row0 = r * tile_rows + d * share
    holder = row0 // tile_cols == c
    square = lax.dynamic_slice_in_dim(a_share, row0 % tile_cols, share, 1)
    a_ii = jnp.sum(jnp.where(jnp.eye(share, dtype=bool), square, 0.0), axis=0)
    a_ii = first_row_of_tile(jnp.where(holder, a_ii, 0.0)[None])[0]
    same = jnp.concatenate([a_diag.reshape(tiles, SUBLANES, LANES), a_ii])
    a_sent = jnp.concatenate(
        [
            jnp.broadcast_to(same[None], (cols, *same.shape)),
            a_panel.reshape(cols, c_share, tile_cols // LANES, LANES).transpose(0, 2, 1, 3),
        ],
        axis=1,
    )
    a_got = exchange(a_sent, "col")
    a_diag = a_got[0, :tiles]
    a_ii = a_got[:, tiles].sum(axis=0)
    a_panel = a_got[0, tiles + 1 :].transpose(1, 0, 2).reshape(c_share, tile_cols)

    swap = [(0, 1), (1, 0)]
    far = lax.ppermute(panels[:PB], "row", swap)
    far_rest = lax.ppermute(panels[PB:], "row", swap)

    near = panels[:PB]
    part = packed(times_transposed(near, near)).reshape(depth, tiles, SUBLANES, LANES)
    part_ii = jnp.sum(panels * panels, axis=1).reshape(depth, share)
    got = exchange(jnp.concatenate([part, first_row_of_tile(part_ii)], axis=1), DEPTH).sum(axis=0)
    diag_ii = a_ii - got[tiles]
    total = jnp.sum(diag_ii * diag_ii)
    piece = jnp.concatenate([a_diag - got[:tiles], jnp.broadcast_to(total, (1, SUBLANES, LANES))])
    mine = to_everyone(piece, DEPTH)
    other = lax.ppermute(mine, "row", swap)
    total = jnp.sum(mine[:, tiles, 0, 0]) + jnp.sum(other[:, tiles, 0, 0])
    diag_norm = jnp.sqrt(total / (rows * tile_rows)).reshape(1)

    top = jnp.where(r == 0, near, far)
    own = lax.dynamic_slice_in_dim(panels, c * c_rows, c_rows, 0)
    c_part = times_transposed(own, top).reshape(depth, c_share, tile_cols)
    c_piece = a_panel - exchange(c_part, DEPTH).sum(axis=0)
    c_all = to_everyone(c_piece, DEPTH).reshape(c_rows, tile_cols)

    first = c * tile_cols
    here = first // tile_rows == r
    half = first % tile_rows // PB
    right = jnp.where(
        here,
        lax.dynamic_slice_in_dim(panels, half * PB, PB, 0),
        jnp.where(half == 0, far, far_rest),
    )
    block = times_transposed(panels, right)
    block = block.reshape(z_size, y_size, share, tile_cols).transpose(1, 0, 2, 3)
    block = exchange(block, "depth_1").sum(axis=0)
    trailing = a_share - exchange(block, "depth_0").sum(axis=0)

    new_panel = solve(r, mine, other, c_all)
    return (trailing, new_panel, diag_norm)


def solution(mesh):
    finer = Mesh(
        mesh.devices.reshape(mesh.shape["row"], mesh.shape["col"], 8, 4),
        ("row", "col", "depth_0", "depth_1"),
    )
    in_specs = (P("row", "col"), P("row", DEPTH))
    out_specs = (P(ROW_DEPTH, "col"), P(("row", "col"), None), P())
    return jax.shard_map(local, mesh=finer, in_specs=in_specs, out_specs=out_specs, check_vma=False)
```

time: 405 us -> 188 us (0.46); the launches traced: 400 us -> 187 us
  blocking collectives: 172 us -> 0 us
  other arithmetic: 124 us -> 11.4 us
  waiting for transfers between devices: 31.2 us -> 68.6 us
  starting transfers between devices: 4.87 us -> 42.1 us
  Pallas kernels: 0 us -> 21.5 us
  between operations: 19 us -> 3.44 us
  local copies, waits for them, and re-layouts: 28.3 us -> 20.3 us
    another operation x17 -> x0, other arithmetic: 120 us -> none  [the longest x14 78.5 us: local(): factor = jnp.linalg.cholesky(diag_block)]
    all_to_all x2 -> x0, blocking collectives: 116 us -> none  [the longest x1 60.7 us: sum_at_owner(): lax.all_to_all(pieces, axis, split_axis=0, concat_axis=0, tiled=True)]
    all_to_all x1 -> x7, waiting for transfers between devices: 0.01 us -> 67.9 us  [exchange(): return lax.all_to_all(pieces, axis, split_axis=0, concat_axis=0, tiled=True)]
    psum x4 -> x0, blocking collectives: 55.9 us -> none  [over_axes(): value = lax.psum(value, axis)]
    all_to_all x1 -> x7, starting transfers between devices: 4.79 us -> 41.5 us  [exchange(): return lax.all_to_all(pieces, axis, split_axis=0, concat_axis=0, tiled=True)]
    all_gather x2 -> x0, waiting for transfers between devices: 31.1 us -> none  [broadcast(): lax.all_gather(value, axis)]
    pallas_call x0 -> x1, Pallas kernels: none -> 21.5 us  [solve(): pl.pallas_call(solve_kernel, out_shape=jax.ShapeDtypeStruct(c_rows.shape,...]
    another operation x17 -> x1, local copies, waits for them, and re-layouts: 13.7 us -> 0.09 us  [first_row_of_tile(): values[:, None, None, :]]
  transfers between devices with their start and end apart: 3 -> 10, of which waited for: 2 -> 6; matrix products, arithmetic and copies ran while one was open for 1% -> 20% of each run, Pallas kernels for 0% -> 12%
where the time goes in v1:
time: 188 us; the launch traced here: 187 us
  waiting for transfers between devices  68.6 us (36%)
  starting transfers between devices  42.1 us (22%)
  Pallas kernels  21.5 us (11%)
  local copies, waits for them, and re-layouts  20.3 us (11%)
  matrix products  19.4 us (10%)
  other arithmetic  11.4 us (6%)
  between operations  3.44 us (2%)
    all_to_all x7, waiting for transfers between devices, exchange(): return lax.all_to_all(pieces, axis, split_axis=0, concat_axis=0, tiled=True)  67.9 us
    all_to_all x7, starting transfers between devices, exchange(): return lax.all_to_all(pieces, axis, split_axis=0, concat_axis=0, tiled=True)  41.5 us
    pallas_call x1, Pallas kernels, solve(): pl.pallas_call(solve_kernel, out_shape=jax.ShapeDtypeStruct(c_rows.shape,...  21.5 us
    dot_general x3, matrix products, times_transposed(): lax.dot_general(left, right, (((1,), (1,)), ((), ())), precision=lax.Prec...  19.4 us
    unnamed x24, local copies, waits for them, and re-layouts  7.7 us
    slice x1, local copies, waits for them, and re-layouts, local(): far_rest = lax.ppermute(panels[PB:], 'row', swap)  4.85 us
  transfers between devices with their start and end apart: 10, of which 6 were waited for; matrix products, arithmetic and copies ran while one was open for 20% of the time, Pallas kernels for 12%

profile of v1, /device:TPU:2, one launch (start us, length us, event | category | flops | bytes accessed | tf_op | source)
XLA Modules:
  0.0 186.8 jit_solution(2290993407914732959)
XLA Ops:
  10.8 5.6 %all-to-all-start.2 = ((f32[4,10,8,128]{3,2,1,0:T(8,128)}), f32[4,10,8,128]{3,2,1,0:T(8,128)S(1)}, u32[]{:S(2)}, u32[]{:S(2)}) async-start(f32[4,10,8,128]{3,2,1,0:T(8,128)} %pad_maximum_fusion), calls=%async_computation.2 | async-start | bytes 327680 | tf_op jit(solution)/shard_map/all_to_all | solution.py:133
  16.4 2.7 %multiply_reduce_fusion = f32[1024]{0:T(1024)S(1)} fusion(f32[1024,1024]{1,0:T(8,128)} %param.3), kind=kLoop, calls=%fused_computation | loop fusion | flops 2096128 | bytes 4198400 | tf_op jit(solution)/shard_map/reduce_sum | solution.py:194
  19.8 3.5 %fusion.24 = f32[512,512]{1,0:T(8,128)S(1)} fusion(f32[1024,1024]{1,0:T(8,128)S(1)} %copy-done), kind=kOutput, calls=%fused_computation.57 | convolution fusion | flops 3221225472 | bytes 3145728 | tf_op jit(solution)/shard_map/dot_general | solution.py:21
  23.6 0.9 select_maximum_fusion
  24.6 10.8 %all-to-all-start.3 = ((f32[32,6,8,128]{3,2,1,0:T(8,128)}), f32[32,6,8,128]{3,2,1,0:T(8,128)S(1)}, u32[]{:S(2)}, u32[]{:S(2)}) async-start(f32[32,6,8,128]{3,2,1,0:T(8,128)} %select_maximum_fusion), calls=%async_computation.3 | async-start | bytes 1572864 | tf_op jit(solution)/shard_map/all_to_all | solution.py:133
  35.3 4.8 %fusion.26 = (f32[512,1024]{1,0:T(8,128)}, f32[512,1024]{1,0:T(8,128)}) fusion(f32[1024,1024]{1,0:T(8,128)} %param.3), kind=kLoop, calls=%fused_computation.59 | loop fusion | bytes 8388608 | tf_op jit(solution)/shard_map/slice | solution.py:190
  40.7 16.8 %all-to-all-done.3 = f32[32,6,8,128]{3,2,1,0:T(8,128)S(1)} async-done(((f32[32,6,8,128]{3,2,1,0:T(8,128)}), f32[32,6,8,128]{3,2,1,0:T(8,128)S(1)}, u32[]{:S(2)}, u32[]{:S(2)}) %all-to-all-start.3) | async-done | bytes 786464 | tf_op jit(solution)/shard_map/all_to_all | solution.py:133
  59.8 5.2 %all-to-all-start.4 = ((f32[32,6,8,128]{3,2,1,0:T(8,128)}), f32[32,6,8,128]{3,2,1,0:T(8,128)S(1)}, u32[]{:S(2)}, u32[]{:S(2)}) async-start(f32[32,6,8,128]{3,2,1,0:T(8,128)} %broadcast_in_dim.30), calls=%async_computation.4 | async-start | bytes 1572864 | tf_op jit(solution)/shard_map/all_to_all | solution.py:133
  65.1 4.7 %fusion.9 = f32[32,8,512]{2,1,0:T(8,128)} fusion(f32[512,1024]{1,0:T(8,128)S(1)} %collective-permute-done, f32[1024,1024]{1,0:T(8,128)} %param.3, s32[]{:T(128)S(6)} %select_n.105, pred[]{:T(512)S(6)} %eq.22), kind=kOutput, calls=%fused_computation.8 | convolution fusion | flops 1611137024 | bytes 5767173 | tf_op jit(solution)/shard_map/dot_general | solution.py:21
  69.8 17.1 %all-to-all-done.4.mine_ref = f32[32,6,8,128]{3,2,1,0:T(8,128)S(1)} async-done(((f32[32,6,8,128]{3,2,1,0:T(8,128)}), f32[32,6,8,128]{3,2,1,0:T(8,128)S(1)}, u32[]{:S(2)}, u32[]{:S(2)}) %all-to-all-start.4) | async-done | bytes 786464 | tf_op jit(solution)/shard_map/all_to_all | solution.py:133
  87.0 5.2 %all-to-all-start.5 = ((f32[32,8,512]{2,1,0:T(8,128)}), f32[32,8,512]{2,1,0:T(8,128)S(1)}, u32[]{:S(2)}, u32[]{:S(2)}) async-start(f32[32,8,512]{2,1,0:T(8,128)} %fusion.9), calls=%async_computation.5 | async-start | bytes 1048576 | tf_op jit(solution)/shard_map/all_to_all | solution.py:133
  92.2 11.1 %fusion.6 = f32[1024,512]{0,1:T(8,128)} fusion(f32[1024,1024]{1,0:T(8,128)} %param.3, f32[512,1024]{1,0:T(8,128)S(1)} %collective-permute-done, f32[512,1024]{1,0:T(8,128)} %collective-permute-done.1, s32[]{:T(128)S(6)} %select_n.90, pred[]{:T(512)S(6)} %eq.19, pred[]{:T(512)S(6)} %eq.18), kind=kOutput, calls=%fused_computation.7 | convolution fusion | flops 6443499520 | bytes 12582918 | tf_op jit(solution)/shard_map/dot_general | solution.py:21
  103.4 1.9 %copy.8 = f32[1024,512]{1,0:T(8,128)S(1)} copy(f32[1024,512]{0,1:T(8,128)} %fusion.6) | data formatting | bytes 4194304 | tf_op jit(solution)/shard_map/dot_general | solution.py:21
  105.3 1.6 copy.9
  106.9 1.6 all-to-all-done.5
  108.4 3.6 %all-to-all-start = ((f32[4,8,32,512]{3,2,1,0:T(8,128)}), f32[4,8,32,512]{3,2,1,0:T(8,128)S(1)}, u32[]{:S(2)}, u32[]{:S(2)}) async-start(f32[4,8,32,512]{3,2,1,0:T(8,128)} %copy.9), calls=%async_computation | async-start | bytes 4194304 | tf_op jit(solution)/shard_map/all_to_all | solution.py:133
  112.8 22.7 %all-to-all-done = f32[4,8,32,512]{3,2,1,0:T(8,128)S(1)} async-done(((f32[4,8,32,512]{3,2,1,0:T(8,128)}), f32[4,8,32,512]{3,2,1,0:T(8,128)S(1)}, u32[]{:S(2)}, u32[]{:S(2)}) %all-to-all-start) | async-done | bytes 2097184 | tf_op jit(solution)/shard_map/all_to_all | solution.py:133
  136.4 7.7 %all-to-all-start.6 = ((f32[32,8,512]{2,1,0:T(8,128)}), f32[32,8,512]{2,1,0:T(8,128)S(1)}, u32[]{:S(2)}, u32[]{:S(2)}) async-start(f32[32,8,512]{2,1,0:T(8,128)} %broadcast_in_dim.31), calls=%async_computation.6 | async-start | bytes 1048576 | tf_op jit(solution)/shard_map/all_to_all | solution.py:133
  144.8 1.0 reduce_sum.90
  146.5 1.6 slice_reduce_fusion
  149.4 9.7 %all-to-all-done.6 = f32[32,8,512]{2,1,0:T(8,128)S(1)} async-done(((f32[32,8,512]{2,1,0:T(8,128)}), f32[32,8,512]{2,1,0:T(8,128)S(1)}, u32[]{:S(2)}, u32[]{:S(2)}) %all-to-all-start.6) | async-done | bytes 524320 | tf_op jit(solution)/shard_map/all_to_all | solution.py:133
  159.1 3.5 %all-to-all-start.1 = ((f32[8,32,512]{2,1,0:T(8,128)}), f32[8,32,512]{2,1,0:T(8,128)S(1)}, u32[]{:S(2)}, u32[]{:S(2)}) async-start(f32[8,32,512]{2,1,0:T(8,128)} %reduce_sum.90), calls=%async_computation.1 | async-start | bytes 1048576 | tf_op jit(solution)/shard_map/all_to_all | solution.py:133
  162.6 21.5 %panel_solve.1 = f32[256,512]{1,0:T(8,128)} custom-call(s32[1]{0:T(128)} %bitcast.3.top_ref, f32[32,6,8,128]{3,2,1,0:T(8,128)} %copy-done.1, f32[32,6,8,128]{3,2,1,0:T(8,128)} %collective-permute-done.2.other_ref, f32[256,512]{1,0:T(8,128)} %bitcast.45), custom_call_target="tpu_custom_call" | custom-call | flops 20000000000 | bytes 3000000 | tf_op jit(solution)/shard_map/panel_solve/pallas_call | solution.py:118
  184.2 1.5 dynamic-slice_subtract_fusion
  (54 shorter events, 17.0 us)
Async XLA Ops:
  10.8 13.8 %all-to-all-start.2 = ((f32[4,10,8,128]{3,2,1,0:T(8,128)}), f32[4,10,8,128]{3,2,1,0:T(8,128)S(1)}, u32[]{:S(2)}, u32[]{:S(2)}) async-start(f32[4,10,8,128]{3,2,1,0:T(8,128)} %pad_maximum_fusion), calls=%async_computation.2 | async-start | bytes 327680 | tf_op jit(solution)/shard_map/all_to_all | solution.py:133
  16.4 3.4 %copy-start = (f32[1024,1024]{1,0:T(8,128)S(1)}, f32[1024,1024]{1,0:T(8,128)}, u32[]{:S(2)}) copy-start(f32[1024,1024]{1,0:T(8,128)} %param.3) | copy-start | bytes 12582916
  24.6 33.0 %copy-start.3 = (f32[4,10,8,128]{3,2,1,0:T(8,128)}, f32[4,10,8,128]{3,2,1,0:T(8,128)S(1)}, u32[]{:S(2)}) copy-start(f32[4,10,8,128]{3,2,1,0:T(8,128)S(1)} %all-to-all-done.2) | copy-start | bytes 491524
  24.6 33.0 %all-to-all-start.3 = ((f32[32,6,8,128]{3,2,1,0:T(8,128)}), f32[32,6,8,128]{3,2,1,0:T(8,128)S(1)}, u32[]{:S(2)}, u32[]{:S(2)}) async-start(f32[32,6,8,128]{3,2,1,0:T(8,128)} %select_maximum_fusion), calls=%async_computation.3 | async-start | bytes 1572864 | tf_op jit(solution)/shard_map/all_to_all | solution.py:133
  40.2 24.9 %collective-permute-start = (f32[512,1024]{1,0:T(8,128)}, f32[512,1024]{1,0:T(8,128)S(1)}, u32[]{:S(2)}, u32[]{:S(2)}) collective-permute-start(f32[512,1024]{1,0:T(8,128)} %get-tuple-element.4), channel_id=1, source_target_pairs={{0,128},{128,0},{1,129},{129,1},{2,130},{130,2},{3,131},{131,3},{4... | collective-permute-start | bytes 6291464 | tf_op jit(solution)/shard_map/ppermute | solution.py:189
  40.2 52.0 %collective-permute-start.1 = (f32[512,1024]{1,0:T(8,128)}, f32[512,1024]{1,0:T(8,128)}, u32[]{:S(2)}, u32[]{:S(2)}) collective-permute-start(f32[512,1024]{1,0:T(8,128)} %get-tuple-element.3), channel_id=1, source_target_pairs={{0,128},{128,0},{1,129},{129,1},{2,130},{130,2},{3,131},{131,3},{4... | collective-permute-start | bytes 6291464 | tf_op jit(solution)/shard_map/ppermute | solution.py:190
  59.8 27.1 %all-to-all-start.4 = ((f32[32,6,8,128]{3,2,1,0:T(8,128)}), f32[32,6,8,128]{3,2,1,0:T(8,128)S(1)}, u32[]{:S(2)}, u32[]{:S(2)}) async-start(f32[32,6,8,128]{3,2,1,0:T(8,128)} %broadcast_in_dim.30), calls=%async_computation.4 | async-start | bytes 1572864 | tf_op jit(solution)/shard_map/all_to_all | solution.py:133
  87.0 57.2 %copy-start.1 = (f32[32,6,8,128]{3,2,1,0:T(8,128)}, f32[32,6,8,128]{3,2,1,0:T(8,128)S(1)}, u32[]{:S(2)}) copy-start(f32[32,6,8,128]{3,2,1,0:T(8,128)S(1)} %all-to-all-done.4.mine_ref) | copy-start | bytes 2359300
  87.0 21.5 %all-to-all-start.5 = ((f32[32,8,512]{2,1,0:T(8,128)}), f32[32,8,512]{2,1,0:T(8,128)S(1)}, u32[]{:S(2)}, u32[]{:S(2)}) async-start(f32[32,8,512]{2,1,0:T(8,128)} %fusion.9), calls=%async_computation.5 | async-start | bytes 1048576 | tf_op jit(solution)/shard_map/all_to_all | solution.py:133
  108.4 27.1 %all-to-all-start = ((f32[4,8,32,512]{3,2,1,0:T(8,128)}), f32[4,8,32,512]{3,2,1,0:T(8,128)S(1)}, u32[]{:S(2)}, u32[]{:S(2)}) async-start(f32[4,8,32,512]{3,2,1,0:T(8,128)} %copy.9), calls=%async_computation | async-start | bytes 4194304 | tf_op jit(solution)/shard_map/all_to_all | solution.py:133
  136.4 22.7 %all-to-all-start.6 = ((f32[32,8,512]{2,1,0:T(8,128)}), f32[32,8,512]{2,1,0:T(8,128)S(1)}, u32[]{:S(2)}, u32[]{:S(2)}) async-start(f32[32,8,512]{2,1,0:T(8,128)} %broadcast_in_dim.31), calls=%async_computation.6 | async-start | bytes 1048576 | tf_op jit(solution)/shard_map/all_to_all | solution.py:133
  144.0 2.5 %collective-permute-start.2 = (f32[32,6,8,128]{3,2,1,0:T(8,128)S(1)}, f32[32,6,8,128]{3,2,1,0:T(8,128)}, u32[]{:S(2)}, u32[]{:S(2)}) collective-permute-start(f32[32,6,8,128]{3,2,1,0:T(8,128)S(1)} %all-to-all-done.4.mine_ref), channel_id=1, source_target_pairs={{0,128},{128,0},{1,129},{129,1},{2,130},{130,2},{3,131},{131,3},{4... | collective-permute-start | bytes 2359304 | tf_op jit(solution)/shard_map/ppermute | solution.py:200
  159.1 3.5 %copy-start.2 = (f32[32,8,512]{2,1,0:T(8,128)}, f32[32,8,512]{2,1,0:T(8,128)S(1)}, u32[]{:S(2)}) copy-start(f32[32,8,512]{2,1,0:T(8,128)S(1)} %all-to-all-done.6) | copy-start | bytes 1572868
  159.1 25.1 %all-to-all-start.1 = ((f32[8,32,512]{2,1,0:T(8,128)}), f32[8,32,512]{2,1,0:T(8,128)S(1)}, u32[]{:S(2)}, u32[]{:S(2)}) async-start(f32[8,32,512]{2,1,0:T(8,128)} %reduce_sum.90), calls=%async_computation.1 | async-start | bytes 1048576 | tf_op jit(solution)/shard_map/all_to_all | solution.py:133
